TPU v7x, 32 devices: a whole 2x2x4 slice. The times are simulated.
32 devices in a mesh: shard: 8 (over y, x, core), width: 4 (over z).
Axes of the slice: x: 2, y: 2, z: 4, core: 2. Of those that a mesh axis runs over, the one named last changes fastest.
Arguments:
- w_up: bfloat16 [12288, 49152], P('shard', 'width'), may hold values from -0.078125 to 0.078125
- low_up: bfloat16 [12288, 64], P('shard'), may hold values from -0.0546875 to 0.0546875
- high_up: bfloat16 [64, 49152], P(None, 'width'), may hold values from -0.75 to 0.75
- norm_train: float32 [12288], P(('shard', 'width')), may hold values from 0.25 to 1.75
- norm_step: float32 [12288], P(('shard', 'width')), may hold values from -0.3 to 0.3
Outputs:
- serve_up: bfloat16 [12288, 49152], P(None, ('width', 'shard'))
- scale_up: float32 [49152], P(('width', 'shard'))
- serve_norm: bfloat16 [12288], replicated
All inputs are finite; a program needn't handle non-finite values. Where the computation divides by a largest or mean magnitude, that divisor is 1e-20 or more.
Results may differ from a plain program's by a relative error of at most 0.001.
Values may be sent and summed in bfloat16 or wider, within the bound.
A program may use at most 256 MiB of HBM per device.

v0:
```python
import functools

import jax
import jax.numpy as jnp
from jax import lax
from jax.experimental import pallas as pl
from jax.experimental.pallas import tpu as pltpu
from jax.sharding import PartitionSpec as P

MESH = pl.DeviceIdType.MESH

mix_rate = 0.5


def tile_of(extent, most):
    for size in range(most, 0, -128):
        if extent % size == 0:
            return size
    return extent


def contract_first(a, b):
    return lax.dot_general(a, b, (((0,), (0,)), ((), ())), preferred_element_type=jnp.float32)


def exchange_kernel(
    n, depth, w_ref, low_ref, high_ref, small_ref,
    g_ref, all_ref, mine_ref, parts_ref,
    send_sem, recv_sem, small_send, small_recv, far_send, far_recv, part_send, part_recv, own_sem,
):
    me = lax.axis_index("shard")
    z = lax.axis_index("width")
    rows = w_ref.shape[0]
    rank = low_ref.shape[0]
    cols = g_ref.shape[1]
    order = sorted(range(1, n), key=lambda k: (bin(k >> 1).count("1"), k))

    def columns(p):
        return pl.ds(pl.multiple_of(p * cols, cols), cols)

    def rows_of(p):
        return pl.ds(pl.multiple_of(p * rows, rows), rows)

    def small_copy(k):
        return pltpu.make_async_remote_copy(
            src_ref=small_ref, dst_ref=all_ref.at[me, z],
            send_sem=small_send.at[k], recv_sem=small_recv.at[k],
            device_id={"shard": me ^ k}, device_id_type=MESH,
        )

    def big_copy(k):
        return pltpu.make_async_remote_copy(
            src_ref=w_ref.at[:, columns(me ^ k)], dst_ref=g_ref.at[rows_of(me), :],
            send_sem=send_sem.at[k], recv_sem=recv_sem.at[k],
            device_id={"shard": me ^ k}, device_id_type=MESH,
        )

    def part_copy(k):
        return pltpu.make_async_remote_copy(
            src_ref=mine_ref.at[:, columns(me ^ k)], dst_ref=parts_ref.at[me],
            send_sem=part_send.at[k], recv_sem=part_recv.at[k],
            device_id={"shard": me ^ k}, device_id_type=MESH,
        )

    def far_copy(k):
        return pltpu.make_async_remote_copy(
            src_ref=all_ref.at[:, z], dst_ref=all_ref.at[:, z],
            send_sem=far_send.at[k], recv_sem=far_recv.at[k],
            device_id={"width": z ^ k}, device_id_type=MESH,
        )

    own_small = pltpu.make_async_copy(small_ref, all_ref.at[me, z], own_sem.at[0])
    own_small.start()
    for k in order:
        small_copy(k).start()
    for k in order:
        big_copy(k).start()

    own_small.wait()
    for k in order:
        small_copy(k).wait()
    for k in range(1, depth):
        far_copy(k).start()

    tile = tile_of(w_ref.shape[1], 512)
    step = tile_of(rows, 256)

    def add_up(w_tile, high_tile, sum_tile):
        total = jnp.zeros((8, tile), jnp.float32)
        for r in range(0, rows, step):
            fresh = w_tile[r:r + step, :].astype(jnp.float32) + mix_rate * contract_first(
                low_ref[:, r:r + step], high_tile[...]
            )
            total = total + jnp.sum(jnp.abs(fresh).reshape(step // 8, 8, tile), axis=0)
        sum_tile[...] = jnp.sum(total, axis=0, keepdims=True)

    pltpu.emit_pipeline(
        add_up,
        grid=(w_ref.shape[1] // tile,),
        in_specs=[
            pl.BlockSpec((rows, tile), lambda j: (0, j)),
            pl.BlockSpec((rank, tile), lambda j: (0, j)),
        ],
        out_specs=[pl.BlockSpec((1, tile), lambda j: (0, j))],
    )(w_ref, high_ref, mine_ref)

    own_part = pltpu.make_async_copy(mine_ref.at[:, columns(me)], parts_ref.at[me], own_sem.at[1])
    own_part.start()
    for k in order:
        part_copy(k).start()

    band = tile_of(rows, 384)

    def take_over(source, target):
        target[...] = source[...]

    pltpu.emit_pipeline(
        take_over,
        grid=(rows // band,),
        in_specs=[pl.BlockSpec((band, cols), lambda i: (i, me))],
        out_specs=[pl.BlockSpec((band, cols), lambda i: (me * (rows // band) + i, 0))],
    )(w_ref, g_ref)

    own_part.wait()
    for k in range(1, depth):
        far_copy(k).wait()
    for k in order:
        part_copy(k).wait()
    for k in order:
        big_copy(k).wait()


def finish_kernel(inner, w_ref, small_ref, high_ref, parts_ref, out_ref, scale_ref):
    rank = high_ref.shape[0]
    height = w_ref.shape[0]
    scale = jnp.sum(parts_ref[...], axis=0) / inner
    scale_ref[...] = scale
    inverse = 1.0 / scale
    step = tile_of(height, 128)
    for r in range(0, height, step):
        fresh = w_ref[r:r + step, :].astype(jnp.float32) + contract_first(
            small_ref[:rank, r:r + step], high_ref[...]
        )
        out_ref[r:r + step, :] = (fresh * inverse).astype(jnp.bfloat16)


def solution(mesh):
    n, depth = mesh.shape["shard"], mesh.shape["width"]

    def per_device(w_up, low_up, high_up, norm_train, norm_step):
        rows, wide = w_up.shape
        rank = low_up.shape[1]
        cols = wide // n
        part = rows // depth
        me = lax.axis_index("shard")
        z = lax.axis_index("width")
        low = low_up.T
        gain = (norm_train + norm_step).astype(jnp.bfloat16).reshape(1, part)
        small = jnp.concatenate(
            [
                lax.dynamic_slice_in_dim(low, z * part, part, axis=1) * jnp.bfloat16(mix_rate),
                jnp.broadcast_to(gain, (16, part)),
            ],
            axis=0,
        )
        high_own = lax.dynamic_slice_in_dim(high_up, me * cols, cols, axis=1)
        any_spec = pl.BlockSpec(memory_space=pl.ANY)
        dma = pltpu.SemaphoreType.DMA
        gathered, everyone, _, parts = pl.pallas_call(
            functools.partial(exchange_kernel, n, depth),
            out_shape=(
                jax.ShapeDtypeStruct((n * rows, cols), jnp.bfloat16),
                jax.ShapeDtypeStruct((n, depth) + small.shape, jnp.bfloat16),
                jax.ShapeDtypeStruct((1, wide), jnp.float32),
                jax.ShapeDtypeStruct((n, 1, cols), jnp.float32),
            ),
            in_specs=[any_spec, pl.BlockSpec(memory_space=pltpu.VMEM), any_spec, any_spec],
            out_specs=(any_spec,) * 4,
            scratch_shapes=[
                dma((n,)), dma((n,)), dma((n,)), dma((n,)), dma((depth,)), dma((depth,)),
                dma((n,)), dma((n,)), dma((2,)),
            ],
            compiler_params=pltpu.CompilerParams(has_side_effects=True),
            name="exchange",
        )(w_up, low, high_up, small)
        serve_up, scale_up = pl.pallas_call(
            functools.partial(finish_kernel, n * rows),
            grid=(n * depth,),
            out_shape=(
                jax.ShapeDtypeStruct((n * rows, cols), jnp.bfloat16),
                jax.ShapeDtypeStruct((1, cols), jnp.float32),
            ),
            in_specs=[
                pl.BlockSpec((part, cols), lambda i: (i, 0)),
                pl.BlockSpec((None, None) + small.shape, lambda i: (i // depth, i % depth, 0, 0)),
                pl.BlockSpec((rank, cols), lambda i: (0, 0)),
                pl.BlockSpec((n, 1, cols), lambda i: (0, 0, 0)),
            ],
            out_specs=(
                pl.BlockSpec((part, cols), lambda i: (i, 0)),
                pl.BlockSpec((1, cols), lambda i: (0, 0)),
            ),
            compiler_params=pltpu.CompilerParams(dimension_semantics=("arbitrary",)),
            name="finish",
        )(gathered, everyone, high_own, parts)
        serve_norm = everyone[:, :, rank, :].reshape(n * rows)
        return serve_up, scale_up.reshape(cols), serve_norm

    placed = (
        P("shard", "width"),
        P("shard", None),
        P(None, "width"),
        P(("shard", "width")),
        P(("shard", "width")),
    )
    return jax.shard_map(
        per_device,
        mesh=mesh,
        in_specs=placed,
        out_specs=(P(None, ("width", "shard")), P(("width", "shard")), P()),
        check_vma=False,
    )
```

profile of v0, /device:TPU:0, one launch (start us, length us, event | category | flops | bytes accessed | tf_op | source)
XLA Modules:
  0.0 473.2 jit_solution(2752227816964252969)
XLA Ops:
  0.6 0.7 add_convert_fusion
  1.3 0.8 multiply_bitcast_fusion
  2.2 0.6 pad_maximum_fusion.small_ref
  2.8 1.6 constant_dynamic-slice_fusion.high_ref
  4.4 422.9 %exchange.1 = (bf16[12288,1536]{1,0:T(8,128)(2,1)}, bf16[8,4,80,384]{3,2,1,0:T(8,128)(2,1)}, f32[1,12288]{1,0:T(1,128)}, f32[8,1,1536]{2,1,0:T(1,128)}) custom-call(bf16[1536,12288]{1,0:T(8,128)(2,1)} %w_ref.1, bf16[64,1536]{1,0:T(8,128)(2,1)} %bitcast.3, bf16[64,12288]{1,0:T(8,128)(2,1)} %high_ref.1, bf16[80,384]{1,0:T(8,128)(2,1)} %pad_maximum_fusion.small_ref), custom_call_target="tpu_custom_call" | custom-call | tf_op jit(solution)/shard_map/exchange/pallas_call | solution.py:169
  427.3 43.0 %finish.1 = (bf16[12288,1536]{1,0:T(8,128)(2,1)}, f32[1,1536]{1,0:T(1,128)}) custom-call(bf16[12288,1536]{1,0:T(8,128)(2,1)} %get-tuple-element.8.w_ref, bf16[8,4,80,384]{3,2,1,0:T(8,128)(2,1)} %get-tuple-element.9.small_ref, bf16[64,1536]{1,0:T(8,128)(2,1)} %constant_dynamic-slice_fusion.high_ref, f32[8,1,1536]{2,1,0:T(1,128)} %get-tuple-element.10.parts_ref), custom_call_target="tpu_custom_call" | custom-call | tf_op jit(solution)/shard_map/finish/pallas_call | solution.py:186
  470.2 1.1 slice_reduce_fusion
  471.3 0.6 reshape_squeeze.3
  471.9 1.3 reduce
  (1 shorter events, 0.0 us)
where the time goes:
time: 475 us; the launch traced here: 473 us
  Pallas kernels  466 us (98%)
    pallas_call x1, Pallas kernels, per_device(): pl.pallas_call(functools.partial(exchange_kernel, n, depth), out_shape=(j...  423 us
    pallas_call x1, Pallas kernels, per_device(): pl.pallas_call(functools.partial(finish_kernel, n * rows), grid=(n * dept...  43 us

commit v1 on v0

v1 whole, which is shorter than its diff:
```python
import functools

import jax
import jax.numpy as jnp
from jax import lax
from jax.experimental import pallas as pl
from jax.experimental.pallas import tpu as pltpu
from jax.sharding import PartitionSpec as P

MESH = pl.DeviceIdType.MESH

mix_rate = 0.5


def tile_of(extent, most):
    for size in range(most, 0, -128):
        if extent % size == 0:
            return size
    return extent


def contract_first(a, b):
    return lax.dot_general(a, b, (((0,), (0,)), ((), ())), preferred_element_type=jnp.float32)


def exchange_kernel(
    n, depth, inner, w_ref, low_ref, high_ref, train_ref, step_ref,
    out_ref, mine_ref, scale_ref, norm_ref,
    small_ref, all_ref, parts_ref, high_own,
    big_send, big_recv, small_send, small_recv, far_send, far_recv,
    pair_send, pair_recv, part_send, part_recv, own_sem,
):
    me = lax.axis_index("shard")
    z = lax.axis_index("width")
    rows = w_ref.shape[0]
    rank = low_ref.shape[0]
    cols = out_ref.shape[1]
    part = rows // depth
    order = sorted(range(1, n), key=lambda k: (bin(k >> 1).count("1"), k))
    near = [k for k in order if bin(k >> 1).count("1") < 2]
    late = [k for k in order if bin(k >> 1).count("1") >= 2]
    chips = [k for k in order if k % 2 == 0]

    def columns(p):
        return pl.ds(pl.multiple_of(p * cols, cols), cols)

    def rows_of(p, q):
        return pl.ds(pl.multiple_of(p * rows + q * part, part), part)

    def big_copy(k, q):
        return pltpu.make_async_remote_copy(
            src_ref=w_ref.at[pl.ds(pl.multiple_of(q * part, part), part), columns(me ^ k)],
            dst_ref=out_ref.at[rows_of(me, q), :],
            send_sem=big_send.at[k, q], recv_sem=big_recv.at[k, q],
            device_id={"shard": me ^ k}, device_id_type=MESH,
        )

    def small_copy(k):
        return pltpu.make_async_remote_copy(
            src_ref=small_ref, dst_ref=all_ref.at[me, z],
            send_sem=small_send.at[k], recv_sem=small_recv.at[k],
            device_id={"shard": me ^ k}, device_id_type=MESH,
        )

    def far_copy(k, j):
        return pltpu.make_async_remote_copy(
            src_ref=all_ref.at[me ^ k, z], dst_ref=all_ref.at[me ^ k, z],
            send_sem=far_send.at[k, j], recv_sem=far_recv.at[k, j],
            device_id={"width": z ^ j}, device_id_type=MESH,
        )

    def pair_copy(k):
        return pltpu.make_async_remote_copy(
            src_ref=all_ref.at[me ^ k], dst_ref=all_ref.at[me ^ k],
            send_sem=pair_send.at[k], recv_sem=pair_recv.at[k],
            device_id={"shard": me ^ 1}, device_id_type=MESH,
        )

    def part_copy(k):
        return pltpu.make_async_remote_copy(
            src_ref=mine_ref.at[:, columns(me ^ k)], dst_ref=parts_ref.at[me],
            send_sem=part_send.at[k], recv_sem=part_recv.at[k],
            device_id={"shard": me ^ k}, device_id_type=MESH,
        )

    for q in range(1):
        for k in near:
            big_copy(k, q).start()

    own_block = pltpu.make_async_copy(
        w_ref.at[:, columns(me)], out_ref.at[pl.ds(pl.multiple_of(me * rows, rows), rows), :], own_sem.at[0]
    )
    own_block.start()
    own_high = pltpu.make_async_copy(high_ref.at[:, columns(me)], high_own, own_sem.at[1])
    own_high.start()

    for j in range(depth):
        @pl.when(z == j)
        def _():
            small_ref[:rank, :] = low_ref[:, j * part:(j + 1) * part] * jnp.bfloat16(mix_rate)
    gain = (train_ref[...] + step_ref[...]).astype(jnp.bfloat16)
    small_ref[rank:, :] = jnp.broadcast_to(gain, (8, part))

    tile = tile_of(w_ref.shape[1], 512)
    step = tile_of(rows, 256)

    def add_up(w_tile, high_tile, sum_tile):
        total = jnp.zeros((8, tile), jnp.float32)
        for r in range(0, rows, step):
            fresh = w_tile[r:r + step, :].astype(jnp.float32) + mix_rate * contract_first(
                low_ref[:, r:r + step], high_tile[...]
            )
            total = total + jnp.sum(jnp.abs(fresh).reshape(step // 8, 8, tile), axis=0)
        sum_tile[...] = jnp.sum(total, axis=0, keepdims=True)

    pltpu.emit_pipeline(
        add_up,
        grid=(w_ref.shape[1] // tile,),
        in_specs=[
            pl.BlockSpec((rows, tile), lambda j: (0, j)),
            pl.BlockSpec((rank, tile), lambda j: (0, j)),
        ],
        out_specs=[pl.BlockSpec((1, tile), lambda j: (0, j))],
    )(w_ref, high_ref, mine_ref)

    own_small = pltpu.make_async_copy(small_ref, all_ref.at[me, z], own_sem.at[2])
    own_small.start()
    own_part = pltpu.make_async_copy(mine_ref.at[:, columns(me)], parts_ref.at[me], own_sem.at[3])
    own_part.start()
    for k in chips:
        small_copy(k).start()
    for k in order:
        part_copy(k).start()
    for q in range(1, depth):
        for k in near:
            big_copy(k, q).start()
    for q in range(depth):
        for k in late:
            big_copy(k, q).start()

    own_small.wait()
    for k in [0] + chips:
        if k:
            small_copy(k).wait()
        for j in range(1, depth):
            far_copy(k, j).start()
    for k in [0] + chips:
        for j in range(1, depth):
            far_copy(k, j).wait()
        pair_copy(k).start()
    own_part.wait()
    for k in order:
        part_copy(k).wait()
    scale = jnp.sum(parts_ref[...], axis=0) / inner
    scale_ref[...] = scale
    inverse = 1.0 / scale
    for k in [0] + chips:
        pair_copy(k).wait()
    own_high.wait()
    own_block.wait()

    for d in range(n):
        for q in range(depth):
            i = d * depth + q
            norm_ref[i * 8:(i + 1) * 8, :] = all_ref[d, q, rank:, :]

    height = tile_of(part, 128)
    width = tile_of(cols, 512)

    def finish(k):
        d = me ^ k

        def piece(q, carry):
            if k:
                big_copy(k, q).wait_recv()
            for r in range(0, part, height):
                here = pl.ds(pl.multiple_of(d * rows + q * part + r, height), height)
                for c in range(0, cols, width):
                    fresh = out_ref[here, c:c + width].astype(jnp.float32) + contract_first(
                        all_ref[d, q, :rank, r:r + height], high_own[:, c:c + width]
                    )
                    out_ref[here, c:c + width] = (fresh * inverse[:, c:c + width]).astype(jnp.bfloat16)
            return carry

        return piece

    for k in [0] + near:
        lax.fori_loop(0, depth, finish(k), 0)
    late_pieces = [finish(k) for k in late]

    def late_round(q, carry):
        for piece in late_pieces:
            piece(q, carry)
        return carry

    lax.fori_loop(0, depth, late_round, 0)

    for q in range(depth):
        for k in order:
            big_copy(k, q).wait_send()


def put_kernel(held_ref, out_ref, sems):
    pieces = sems.shape[0]
    size = held_ref.shape[0] // pieces
    copies = [
        pltpu.make_async_copy(held_ref.at[i * size:(i + 1) * size, :], out_ref.at[i * size:(i + 1) * size, :], sems.at[i])
        for i in range(pieces)
    ]
    for copy in copies:
        copy.start()
    for copy in copies:
        copy.wait()


def tail_kernel(scale_in, norm_in, scale_ref, norm_ref):
    scale_ref[...] = scale_in[...].reshape(scale_ref.shape)
    part = norm_in.shape[1]
    for i in range(norm_in.shape[0] // 8):
        norm_ref[i * part:(i + 1) * part] = norm_in[i * 8:i * 8 + 1, :].reshape(part)


def solution(mesh):
    n, depth = mesh.shape["shard"], mesh.shape["width"]

    def per_device(w_up, low_up, high_up, norm_train, norm_step):
        rows, wide = w_up.shape
        rank = low_up.shape[1]
        cols = wide // n
        part = rows // depth
        any_spec = pl.BlockSpec(memory_space=pl.ANY)
        vmem_spec = pl.BlockSpec(memory_space=pltpu.VMEM)
        dma = pltpu.SemaphoreType.DMA
        held, _, scale, norm = pl.pallas_call(
            functools.partial(exchange_kernel, n, depth, n * rows),
            out_shape=(
                pltpu.VMEM((n * rows, cols), jnp.bfloat16),
                jax.ShapeDtypeStruct((1, wide), jnp.float32),
                jax.ShapeDtypeStruct((1, cols), jnp.float32),
                jax.ShapeDtypeStruct((n * depth * 8, part), jnp.bfloat16),
            ),
            in_specs=[any_spec, vmem_spec, any_spec, vmem_spec, vmem_spec],
            out_specs=(vmem_spec, any_spec, vmem_spec, vmem_spec),
            scratch_shapes=[
                pltpu.VMEM((rank + 8, part), jnp.bfloat16),
                pltpu.VMEM((n, depth, rank + 8, part), jnp.bfloat16),
                pltpu.VMEM((n, 1, cols), jnp.float32),
                pltpu.VMEM((rank, cols), jnp.bfloat16),
                dma((n, depth)), dma((n, depth)), dma((n,)), dma((n,)), dma((n, depth)), dma((n, depth)),
                dma((n,)), dma((n,)), dma((n,)), dma((n,)), dma((4,)),
            ],
            compiler_params=pltpu.CompilerParams(has_side_effects=True, vmem_limit_bytes=24 * 2**20),
            name="exchange",
        )(w_up, low_up.T, high_up, norm_train.reshape(1, part), norm_step.reshape(1, part))
        serve_up = pl.pallas_call(
            put_kernel,
            out_shape=jax.ShapeDtypeStruct((n * rows, cols), jnp.bfloat16),
            in_specs=[vmem_spec],
            out_specs=any_spec,
            scratch_shapes=[dma((8,))],
            compiler_params=pltpu.CompilerParams(vmem_limit_bytes=4 * 2**20),
            name="put",
        )(held)
        serve_up, scale, norm = lax.optimization_barrier((serve_up, scale, norm))
        scale_up, serve_norm = pl.pallas_call(
            tail_kernel,
            out_shape=(
                jax.ShapeDtypeStruct((cols,), jnp.float32),
                jax.ShapeDtypeStruct((n * rows,), jnp.bfloat16),
            ),
            in_specs=[vmem_spec, vmem_spec],
            out_specs=(vmem_spec, vmem_spec),
            compiler_params=pltpu.CompilerParams(vmem_limit_bytes=4 * 2**20),
            name="tail",
        )(scale, norm)
        return serve_up, scale_up, serve_norm

    placed = (
        P("shard", "width"),
        P("shard", None),
        P(None, "width"),
        P(("shard", "width")),
        P(("shard", "width")),
    )
    return jax.shard_map(
        per_device,
        mesh=mesh,
        in_specs=placed,
        out_specs=(P(None, ("width", "shard")), P(("width", "shard")), P()),
        check_vma=False,
    )
```

time: 475 us -> 439 us (0.924)
  Pallas kernels: 466 us -> 435 us
    pallas_call x2 -> x3, Pallas kernels: 466 us -> 435 us  [the longest x1 422 us: per_device(): pl.pallas_call(functools.partial(exchange_kernel, n, depth, n * rows), ou...]
where the time goes in v1:
time: 439 us; the launch traced here: 438 us
  Pallas kernels  435 us (99%)
    pallas_call x1, Pallas kernels, per_device(): pl.pallas_call(functools.partial(exchange_kernel, n, depth, n * rows), ou...  422 us
    pallas_call x1, Pallas kernels, per_device(): pl.pallas_call(put_kernel, out_shape=jax.ShapeDtypeStruct((n * rows, cols...  12.3 us

profile of v1, /device:TPU:0, one launch (start us, length us, event | category | flops | bytes accessed | tf_op | source)
XLA Modules:
  0.0 437.8 jit_solution(17874304733518024520)
XLA Ops:
  0.6 1.2 reshape.12.train_ref
  1.9 1.2 reshape.13.step_ref
  3.1 421.6 %exchange.1 = (bf16[12288,1536]{1,0:T(8,128)(2,1)S(1)}, f32[1,12288]{1,0:T(1,128)}, f32[1,1536]{1,0:T(1,128)}, bf16[256,384]{1,0:T(8,128)(2,1)}) custom-call(bf16[1536,12288]{1,0:T(8,128)(2,1)} %w_ref.1, bf16[64,1536]{1,0:T(8,128)(2,1)} %bitcast.1, bf16[64,12288]{1,0:T(8,128)(2,1)} %high_ref.1, f32[1,384]{1,0:T(1,128)} %reshape.12.train_ref, ...), custom_call_target="tpu_custom_call" | custom-call | tf_op jit(solution)/shard_map/exchange/pallas_call | solution.py:234
  424.8 0.0 copy-start
  424.8 0.0 copy-start.1
  424.8 12.3 %put.1 = bf16[12288,1536]{1,0:T(8,128)(2,1)} custom-call(bf16[12288,1536]{1,0:T(8,128)(2,1)S(1)} %get-tuple-element.11.held_ref), custom_call_target="tpu_custom_call" | custom-call | tf_op jit(solution)/shard_map/put/pallas_call | solution.py:255
  437.1 0.0 copy-done
  437.1 0.0 copy-done.1
  437.1 0.7 tail.1
Async XLA Ops:
  424.8 12.4 %copy-start = (bf16[256,384]{1,0:T(8,128)(2,1)S(1)}, bf16[256,384]{1,0:T(8,128)(2,1)}, u32[]{:S(2)}) copy-start(bf16[256,384]{1,0:T(8,128)(2,1)} %get-tuple-element.16.norm_in) | copy-start | bytes 589828
  424.8 12.4 %copy-start.1 = (f32[1,1536]{1,0:T(1,128)S(1)}, f32[1,1536]{1,0:T(1,128)}, u32[]{:S(2)}) copy-start(f32[1,1536]{1,0:T(1,128)} %get-tuple-element.15.scale_in) | copy-start | bytes 18436

commit v2 on v1

--- a/solution.py
+++ b/solution.py
@@ -24,11 +24,11 @@
 
 
 def exchange_kernel(
-    n, depth, inner, w_ref, low_ref, high_ref, train_ref, step_ref,
-    out_ref, mine_ref, scale_ref, norm_ref,
+    n, depth, held_back, inner, w_ref, low_ref, high_ref, train_ref, step_ref,
+    out_ref, mine_ref, scale_ref, norm_ref, low_late_ref,
     small_ref, all_ref, parts_ref, high_own,
     big_send, big_recv, small_send, small_recv, far_send, far_recv,
-    pair_send, pair_recv, part_send, part_recv, own_sem,
+    pair_send, pair_recv, part_send, part_recv, unit_send, unit_recv, own_sem,
 ):
     me = lax.axis_index("shard")
     z = lax.axis_index("width")
@@ -36,9 +36,13 @@
     rank = low_ref.shape[0]
     cols = out_ref.shape[1]
     part = rows // depth
+    height = tile_of(part, 128)
+    width = tile_of(cols, 512)
+    units = rows // height
+    far = n - 2
     order = sorted(range(1, n), key=lambda k: (bin(k >> 1).count("1"), k))
     near = [k for k in order if bin(k >> 1).count("1") < 2]
-    late = [k for k in order if bin(k >> 1).count("1") >= 2]
+    late = [k for k in order if bin(k >> 1).count("1") >= 2 and k != far]
     chips = [k for k in order if k % 2 == 0]
 
     def columns(p):
@@ -55,6 +59,14 @@
             device_id={"shard": me ^ k}, device_id_type=MESH,
         )
 
+    def unit_copy(u):
+        return pltpu.make_async_remote_copy(
+            src_ref=w_ref.at[u * height:(u + 1) * height, columns(me ^ far)],
+            dst_ref=out_ref.at[pl.ds(pl.multiple_of(me * rows + u * height, height), height), :],
+            send_sem=unit_send.at[u], recv_sem=unit_recv.at[u],
+            device_id={"shard": me ^ far}, device_id_type=MESH,
+        )
+
     def small_copy(k):
         return pltpu.make_async_remote_copy(
             src_ref=small_ref, dst_ref=all_ref.at[me, z],
@@ -82,6 +94,13 @@
             send_sem=part_send.at[k], recv_sem=part_recv.at[k],
             device_id={"shard": me ^ k}, device_id_type=MESH,
         )
+
+    barrier = pltpu.get_barrier_semaphore()
+    for k in order:
+        pl.semaphore_signal(barrier, inc=1, device_id={"shard": me ^ k}, device_id_type=MESH)
+    for j in range(1, depth):
+        pl.semaphore_signal(barrier, inc=1, device_id={"width": z ^ j}, device_id_type=MESH)
+    pl.semaphore_wait(barrier, len(order) + depth - 1)
 
     for q in range(1):
         for k in near:
@@ -98,8 +117,8 @@
         @pl.when(z == j)
         def _():
             small_ref[:rank, :] = low_ref[:, j * part:(j + 1) * part] * jnp.bfloat16(mix_rate)
-    gain = (train_ref[...] + step_ref[...]).astype(jnp.bfloat16)
-    small_ref[rank:, :] = jnp.broadcast_to(gain, (8, part))
+    gain = (train_ref[...] + step_ref[...]).reshape(1, part)
+    small_ref[rank:, :] = jnp.broadcast_to(gain, (8, part)).astype(jnp.bfloat16)
 
     tile = tile_of(w_ref.shape[1], 512)
     step = tile_of(rows, 256)
@@ -137,6 +156,13 @@
     for q in range(depth):
         for k in late:
             big_copy(k, q).start()
+    for u in range(units - held_back):
+        unit_copy(u).start()
+
+    @pl.when(me % 2 == 1)
+    def _():
+        for u in range(units - held_back, units):
+            unit_copy(u).start()
 
     own_small.wait()
     for k in [0] + chips:
@@ -164,22 +190,20 @@
             i = d * depth + q
             norm_ref[i * 8:(i + 1) * 8, :] = all_ref[d, q, rank:, :]
 
-    height = tile_of(part, 128)
-    width = tile_of(cols, 512)
+    def finish_rows(d, q, r):
+        here = pl.ds(pl.multiple_of(d * rows + q * part + r, height), height)
+        for c in range(0, cols, width):
+            fresh = out_ref[here, c:c + width].astype(jnp.float32) + contract_first(
+                all_ref[d, q, :rank, r:r + height], high_own[:, c:c + width]
+            )
+            out_ref[here, c:c + width] = (fresh * inverse[:, c:c + width]).astype(jnp.bfloat16)
 
     def finish(k):
-        d = me ^ k
-
         def piece(q, carry):
             if k:
                 big_copy(k, q).wait_recv()
             for r in range(0, part, height):
-                here = pl.ds(pl.multiple_of(d * rows + q * part + r, height), height)
-                for c in range(0, cols, width):
-                    fresh = out_ref[here, c:c + width].astype(jnp.float32) + contract_first(
-                        all_ref[d, q, :rank, r:r + height], high_own[:, c:c + width]
-                    )
-                    out_ref[here, c:c + width] = (fresh * inverse[:, c:c + width]).astype(jnp.bfloat16)
+                finish_rows(me ^ k, q, r)
             return carry
 
         return piece
@@ -194,10 +218,75 @@
         return carry
 
     lax.fori_loop(0, depth, late_round, 0)
-
-    for q in range(depth):
-        for k in order:
+    per = part // height
+
+    def finish_unit(u):
+        unit_copy(u).wait_recv()
+        finish_rows(me ^ far, u // per, u % per * height)
+
+    for i in range(held_back):
+        u = units - held_back + i
+        low_late_ref[:, i * height:(i + 1) * height] = all_ref[
+            me ^ far, u // per, :rank, u % per * height:u % per * height + height
+        ]
+    for u in range(units - held_back):
+        finish_unit(u)
+    for k in near + late:
+        for q in range(depth):
             big_copy(k, q).wait_send()
+    for u in range(units - held_back):
+        unit_copy(u).wait_send()
+
+    @pl.when(me % 2 == 1)
+    def _():
+        for u in range(units - held_back, units):
+            finish_unit(u)
+        for u in range(units - held_back, units):
+            unit_copy(u).wait_send()
+
+
+def second_kernel(n, held_back, w_ref, low_ref, high_ref, scale_ref, got_ref, high_own, send_sem, recv_sem, own_sem):
+    me = lax.axis_index("shard")
+    rows = w_ref.shape[0]
+    cols = got_ref.shape[1]
+    height = got_ref.shape[0] // held_back
+    width = tile_of(cols, 512)
+    units = rows // height
+    far = n - 2
+
+    def columns(p):
+        return pl.ds(pl.multiple_of(p * cols, cols), cols)
+
+    def unit_copy(i):
+        u = units - held_back + i
+        return pltpu.make_async_remote_copy(
+            src_ref=w_ref.at[u * height:(u + 1) * height, columns(me ^ far)],
+            dst_ref=got_ref.at[i * height:(i + 1) * height, :],
+            send_sem=send_sem.at[i], recv_sem=recv_sem.at[i],
+            device_id={"shard": me ^ far}, device_id_type=MESH,
+        )
+
+    @pl.when(me % 2 == 0)
+    def _():
+        barrier = pltpu.get_barrier_semaphore()
+        pl.semaphore_signal(barrier, inc=1, device_id={"shard": me ^ far}, device_id_type=MESH)
+        own_high = pltpu.make_async_copy(high_ref.at[:, columns(me)], high_own, own_sem)
+        own_high.start()
+        pl.semaphore_wait(barrier, 1)
+        for i in range(held_back):
+            unit_copy(i).start()
+        inverse = 1.0 / scale_ref[...]
+        own_high.wait()
+        for i in range(held_back):
+            unit_copy(i).wait_recv()
+            here = slice(i * height, (i + 1) * height)
+            for c in range(0, cols, width):
+                fresh = got_ref[here, c:c + width].astype(jnp.float32) + contract_first(
+                    low_ref[:, here], high_own[:, c:c + width]
+                )
+                got_ref[here, c:c + width] = (fresh * inverse[:, c:c + width]).astype(jnp.bfloat16)
+        for i in range(held_back):
+            unit_copy(i).wait_send()
 
 
 def put_kernel(held_ref, out_ref, sems):
@@ -213,11 +302,25 @@
         copy.wait()
 
 
-def tail_kernel(scale_in, norm_in, scale_ref, norm_ref):
+def tail_kernel(n, put_ref, got_ref, scale_in, norm_in, out_ref, scale_ref, norm_ref, sem):
+    me = lax.axis_index("shard")
+    late = got_ref.shape[0]
+    rows = out_ref.shape[0] // n
+    last = pl.ds(pl.multiple_of((me ^ (n - 2)) * rows + (rows - late), 8), late)
+    copy = pltpu.make_async_copy(got_ref, out_ref.at[last, :], sem)
+
+    @pl.when(me % 2 == 0)
+    def _():
+        copy.start()
+
     scale_ref[...] = scale_in[...].reshape(scale_ref.shape)
     part = norm_in.shape[1]
     for i in range(norm_in.shape[0] // 8):
         norm_ref[i * part:(i + 1) * part] = norm_in[i * 8:i * 8 + 1, :].reshape(part)
+
+    @pl.when(me % 2 == 0)
+    def _():
+        copy.wait()
 
 
 def solution(mesh):
@@ -228,30 +331,34 @@
         rank = low_up.shape[1]
         cols = wide // n
         part = rows // depth
+        height = tile_of(part, 128)
+        units = rows // height
+        held_back = units // 3
         any_spec = pl.BlockSpec(memory_space=pl.ANY)
         vmem_spec = pl.BlockSpec(memory_space=pltpu.VMEM)
         dma = pltpu.SemaphoreType.DMA
-        held, _, scale, norm = pl.pallas_call(
-            functools.partial(exchange_kernel, n, depth, n * rows),
+        held, _, scale, norm, low_late = pl.pallas_call(
+            functools.partial(exchange_kernel, n, depth, held_back, n * rows),
             out_shape=(
                 pltpu.VMEM((n * rows, cols), jnp.bfloat16),
                 jax.ShapeDtypeStruct((1, wide), jnp.float32),
                 jax.ShapeDtypeStruct((1, cols), jnp.float32),
                 jax.ShapeDtypeStruct((n * depth * 8, part), jnp.bfloat16),
+                jax.ShapeDtypeStruct((rank, held_back * height), jnp.bfloat16),
             ),
             in_specs=[any_spec, vmem_spec, any_spec, vmem_spec, vmem_spec],
-            out_specs=(vmem_spec, any_spec, vmem_spec, vmem_spec),
+            out_specs=(vmem_spec, any_spec, vmem_spec, vmem_spec, vmem_spec),
             scratch_shapes=[
                 pltpu.VMEM((rank + 8, part), jnp.bfloat16),
                 pltpu.VMEM((n, depth, rank + 8, part), jnp.bfloat16),
                 pltpu.VMEM((n, 1, cols), jnp.float32),
                 pltpu.VMEM((rank, cols), jnp.bfloat16),
                 dma((n, depth)), dma((n, depth)), dma((n,)), dma((n,)), dma((n, depth)), dma((n, depth)),
-                dma((n,)), dma((n,)), dma((n,)), dma((n,)), dma((4,)),
+                dma((n,)), dma((n,)), dma((n,)), dma((n,)), dma((units,)), dma((units,)), dma((4,)),
             ],
-            compiler_params=pltpu.CompilerParams(has_side_effects=True, vmem_limit_bytes=24 * 2**20),
+            compiler_params=pltpu.CompilerParams(collective_id=0, has_side_effects=True, vmem_limit_bytes=24 * 2**20),
             name="exchange",
-        )(w_up, low_up.T, high_up, norm_train.reshape(1, part), norm_step.reshape(1, part))
+        )(w_up, low_up.T, high_up, norm_train, norm_step)
         serve_up = pl.pallas_call(
             put_kernel,
             out_shape=jax.ShapeDtypeStruct((n * rows, cols), jnp.bfloat16),
@@ -261,18 +368,34 @@
             compiler_params=pltpu.CompilerParams(vmem_limit_bytes=4 * 2**20),
             name="put",
         )(held)
-        serve_up, scale, norm = lax.optimization_barrier((serve_up, scale, norm))
-        scale_up, serve_norm = pl.pallas_call(
-            tail_kernel,
+        serve_up, scale, norm, low_late = lax.optimization_barrier((serve_up, scale, norm, low_late))
+        got = pl.pallas_call(
+            functools.partial(second_kernel, n, held_back),
+            out_shape=pltpu.VMEM((held_back * height, cols), jnp.bfloat16),
+            in_specs=[any_spec, vmem_spec, any_spec, vmem_spec],
+            out_specs=vmem_spec,
+            scratch_shapes=[
+                pltpu.VMEM((rank, cols), jnp.bfloat16), dma((held_back,)), dma((held_back,)), dma,
+            ],
+            compiler_params=pltpu.CompilerParams(
+                collective_id=1, has_side_effects=True, vmem_limit_bytes=16 * 2**20
+            ),
+            name="second",
+        )(w_up, low_late, high_up, scale)
+        serve_up, scale_up, serve_norm = pl.pallas_call(
+            functools.partial(tail_kernel, n),
             out_shape=(
+                jax.ShapeDtypeStruct((n * rows, cols), jnp.bfloat16),
                 jax.ShapeDtypeStruct((cols,), jnp.float32),
                 jax.ShapeDtypeStruct((n * rows,), jnp.bfloat16),
             ),
-            in_specs=[vmem_spec, vmem_spec],
-            out_specs=(vmem_spec, vmem_spec),
-            compiler_params=pltpu.CompilerParams(vmem_limit_bytes=4 * 2**20),
+            in_specs=[any_spec, vmem_spec, vmem_spec, vmem_spec],
+            out_specs=(any_spec, vmem_spec, vmem_spec),
+            scratch_shapes=[dma],
+            input_output_aliases={0: 0},
+            compiler_params=pltpu.CompilerParams(vmem_limit_bytes=8 * 2**20),
             name="tail",
-        )(scale, norm)
+        )(serve_up, got, scale, norm)
         return serve_up, scale_up, serve_norm
 
     placed = (

time: 439 us -> 424 us (0.966)
  Pallas kernels: 435 us -> 423 us
    pallas_call x2 -> x3, Pallas kernels: 422 us -> 410 us  [the longest x1 387 us: per_device(): pl.pallas_call(functools.partial(exchange_kernel, n, depth, held_back, n...]
where the time goes in v2:
time: 424 us
  Pallas kernels  423 us (100%)
    pallas_call x1, Pallas kernels, per_device(): pl.pallas_call(functools.partial(exchange_kernel, n, depth, held_back, n...  387 us
    pallas_call x1, Pallas kernels, per_device(): pl.pallas_call(functools.partial(second_kernel, n, held_back), out_shape=...  21.9 us
    pallas_call x1, Pallas kernels, per_device(): pl.pallas_call(put_kernel, out_shape=jax.ShapeDtypeStruct((n * rows, cols...  12.3 us

profile of v2, /device:TPU:0, one launch (start us, length us, event | category | flops | bytes accessed | tf_op | source)
XLA Modules:
  0.0 423.5 jit_solution(3026282425862851029)
XLA Ops:
  0.6 386.8 %exchange.1 = (bf16[12288,1536]{1,0:T(8,128)(2,1)S(1)}, f32[1,12288]{1,0:T(1,128)}, f32[1,1536]{1,0:T(1,128)}, bf16[256,384]{1,0:T(8,128)(2,1)}, bf16[64,512]{1,0:T(8,128)(2,1)}) custom-call(bf16[1536,12288]{1,0:T(8,128)(2,1)} %w_ref.3, bf16[64,1536]{1,0:T(8,128)(2,1)} %bitcast.1, bf16[64,12288]{1,0:T(8,128)(2,1)} %high_ref.3, f32[384]{0:T(512)} %train_ref.1, ...), custom_call_target="tpu_custom_call" | custom-call | tf_op jit(solution)/shard_map/exchange/pallas_call | solution.py:340
  387.4 0.0 copy-start
  387.4 0.0 copy-start.2
  387.4 0.0 copy-start.3
  387.4 12.3 %put.1.put_ref = bf16[12288,1536]{1,0:T(8,128)(2,1)} custom-call(bf16[12288,1536]{1,0:T(8,128)(2,1)S(1)} %get-tuple-element.11.held_ref), custom_call_target="tpu_custom_call" | custom-call | tf_op jit(solution)/shard_map/put/pallas_call | solution.py:362
  399.8 0.0 copy-done
  399.8 0.0 copy-done.2
  399.8 0.0 copy-done.3
  399.8 0.0 copy-start.1
  399.8 21.9 %second.1.got_ref = bf16[512,1536]{1,0:T(8,128)(2,1)S(1)} custom-call(bf16[1536,12288]{1,0:T(8,128)(2,1)} %w_ref.3, bf16[64,512]{1,0:T(8,128)(2,1)S(1)} %copy-done.2, bf16[64,12288]{1,0:T(8,128)(2,1)S(1)} %copy-done, f32[1,1536]{1,0:T(1,128)S(1)} %copy-done.3), custom_call_target="tpu_custom_call" | custom-call | tf_op jit(solution)/shard_map/second/pallas_call | solution.py:372
  421.8 0.0 copy-done.1
  421.8 1.8 tail.1
Async XLA Ops:
  387.4 12.4 %copy-start = (bf16[64,12288]{1,0:T(8,128)(2,1)S(1)}, bf16[64,12288]{1,0:T(8,128)(2,1)}, u32[]{:S(2)}) copy-start(bf16[64,12288]{1,0:T(8,128)(2,1)} %high_ref.3) | copy-start | bytes 4718596
  387.4 12.4 %copy-start.2 = (bf16[64,512]{1,0:T(8,128)(2,1)S(1)}, bf16[64,512]{1,0:T(8,128)(2,1)}, u32[]{:S(2)}) copy-start(bf16[64,512]{1,0:T(8,128)(2,1)} %get-tuple-element.16.low_ref) | copy-start | bytes 196612
  387.4 12.4 %copy-start.3 = (f32[1,1536]{1,0:T(1,128)S(1)}, f32[1,1536]{1,0:T(1,128)}, u32[]{:S(2)}) copy-start(f32[1,1536]{1,0:T(1,128)} %get-tuple-element.17.scale_ref.scale_in) | copy-start | bytes 18436
  399.8 22.0 %copy-start.1 = (bf16[256,384]{1,0:T(8,128)(2,1)S(1)}, bf16[256,384]{1,0:T(8,128)(2,1)}, u32[]{:S(2)}) copy-start(bf16[256,384]{1,0:T(8,128)(2,1)} %get-tuple-element.18.norm_in) | copy-start | bytes 589828

commit v3 on v2

--- a/solution.py
+++ b/solution.py
@@ -24,9 +24,9 @@
 
 
 def exchange_kernel(
-    n, depth, held_back, inner, w_ref, low_ref, high_ref, train_ref, step_ref,
+    n, depth, held_back, inner, w_ref, low_in, high_ref, train_in, step_in,
     out_ref, mine_ref, scale_ref, norm_ref, low_late_ref,
-    small_ref, all_ref, parts_ref, high_own,
+    low_ref, train_ref, step_ref, small_ref, all_ref, parts_ref, high_own,
     big_send, big_recv, small_send, small_recv, far_send, far_recv,
     pair_send, pair_recv, part_send, part_recv, unit_send, unit_recv, own_sem,
 ):
@@ -100,6 +100,13 @@
         pl.semaphore_signal(barrier, inc=1, device_id={"shard": me ^ k}, device_id_type=MESH)
     for j in range(1, depth):
         pl.semaphore_signal(barrier, inc=1, device_id={"width": z ^ j}, device_id_type=MESH)
+    taken = [
+        pltpu.make_async_copy(low_in, low_ref, own_sem.at[4]),
+        pltpu.make_async_copy(train_in, train_ref, own_sem.at[5]),
+        pltpu.make_async_copy(step_in, step_ref, own_sem.at[6]),
+    ]
+    for copy in taken:
+        copy.start()
     pl.semaphore_wait(barrier, len(order) + depth - 1)
 
     for q in range(1):
@@ -113,6 +120,8 @@
     own_high = pltpu.make_async_copy(high_ref.at[:, columns(me)], high_own, own_sem.at[1])
     own_high.start()
 
+    for copy in taken:
+        copy.wait()
     for j in range(depth):
         @pl.when(z == j)
         def _():
@@ -302,24 +311,23 @@
         copy.wait()
 
 
-def tail_kernel(n, put_ref, got_ref, scale_in, norm_in, out_ref, scale_ref, norm_ref, sem):
+def side_kernel(scale_in, norm_in, scale_ref, norm_ref):
+    scale_ref[...] = scale_in[...].reshape(scale_ref.shape)
+    part = norm_in.shape[1]
+    for i in range(norm_in.shape[0] // 8):
+        norm_ref[i * part:(i + 1) * part] = norm_in[i * 8:i * 8 + 1, :].reshape(part)
+
+
+def tail_kernel(n, put_ref, got_ref, out_ref, sem):
     me = lax.axis_index("shard")
     late = got_ref.shape[0]
     rows = out_ref.shape[0] // n
     last = pl.ds(pl.multiple_of((me ^ (n - 2)) * rows + (rows - late), 8), late)
-    copy = pltpu.make_async_copy(got_ref, out_ref.at[last, :], sem)
 
     @pl.when(me % 2 == 0)
     def _():
+        copy = pltpu.make_async_copy(got_ref, out_ref.at[last, :], sem)
         copy.start()
-
-    scale_ref[...] = scale_in[...].reshape(scale_ref.shape)
-    part = norm_in.shape[1]
-    for i in range(norm_in.shape[0] // 8):
-        norm_ref[i * part:(i + 1) * part] = norm_in[i * 8:i * 8 + 1, :].reshape(part)
-
-    @pl.when(me % 2 == 0)
-    def _():
         copy.wait()
 
 
@@ -333,7 +341,7 @@
         part = rows // depth
         height = tile_of(part, 128)
         units = rows // height
-        held_back = units // 3
+        held_back = max(1, units // 2)
         any_spec = pl.BlockSpec(memory_space=pl.ANY)
         vmem_spec = pl.BlockSpec(memory_space=pltpu.VMEM)
         dma = pltpu.SemaphoreType.DMA
@@ -346,15 +354,18 @@
                 jax.ShapeDtypeStruct((n * depth * 8, part), jnp.bfloat16),
                 jax.ShapeDtypeStruct((rank, held_back * height), jnp.bfloat16),
             ),
-            in_specs=[any_spec, vmem_spec, any_spec, vmem_spec, vmem_spec],
+            in_specs=[any_spec] * 5,
             out_specs=(vmem_spec, any_spec, vmem_spec, vmem_spec, vmem_spec),
             scratch_shapes=[
+                pltpu.VMEM((rank, rows), jnp.bfloat16),
+                pltpu.VMEM((part,), jnp.float32),
+                pltpu.VMEM((part,), jnp.float32),
                 pltpu.VMEM((rank + 8, part), jnp.bfloat16),
                 pltpu.VMEM((n, depth, rank + 8, part), jnp.bfloat16),
                 pltpu.VMEM((n, 1, cols), jnp.float32),
                 pltpu.VMEM((rank, cols), jnp.bfloat16),
                 dma((n, depth)), dma((n, depth)), dma((n,)), dma((n,)), dma((n, depth)), dma((n, depth)),
-                dma((n,)), dma((n,)), dma((n,)), dma((n,)), dma((units,)), dma((units,)), dma((4,)),
+                dma((n,)), dma((n,)), dma((n,)), dma((n,)), dma((units,)), dma((units,)), dma((7,)),
             ],
             compiler_params=pltpu.CompilerParams(collective_id=0, has_side_effects=True, vmem_limit_bytes=24 * 2**20),
             name="exchange",
@@ -369,6 +380,18 @@
             name="put",
         )(held)
         serve_up, scale, norm, low_late = lax.optimization_barrier((serve_up, scale, norm, low_late))
+        scale_up, serve_norm = pl.pallas_call(
+            side_kernel,
+            out_shape=(
+                jax.ShapeDtypeStruct((cols,), jnp.float32),
+                jax.ShapeDtypeStruct((n * rows,), jnp.bfloat16),
+            ),
+            in_specs=[vmem_spec, vmem_spec],
+            out_specs=(vmem_spec, vmem_spec),
+            compiler_params=pltpu.CompilerParams(vmem_limit_bytes=4 * 2**20),
+            name="side",
+        )(scale, norm)
+        scale, low_late, scale_up, serve_norm = lax.optimization_barrier((scale, low_late, scale_up, serve_norm))
         got = pl.pallas_call(
             functools.partial(second_kernel, n, held_back),
             out_shape=pltpu.VMEM((held_back * height, cols), jnp.bfloat16),
@@ -382,20 +405,16 @@
             ),
             name="second",
         )(w_up, low_late, high_up, scale)
-        serve_up, scale_up, serve_norm = pl.pallas_call(
+        serve_up = pl.pallas_call(
             functools.partial(tail_kernel, n),
-            out_shape=(
-                jax.ShapeDtypeStruct((n * rows, cols), jnp.bfloat16),
-                jax.ShapeDtypeStruct((cols,), jnp.float32),
-                jax.ShapeDtypeStruct((n * rows,), jnp.bfloat16),
-            ),
-            in_specs=[any_spec, vmem_spec, vmem_spec, vmem_spec],
-            out_specs=(any_spec, vmem_spec, vmem_spec),
+            out_shape=jax.ShapeDtypeStruct((n * rows, cols), jnp.bfloat16),
+            in_specs=[any_spec, vmem_spec],
+            out_specs=any_spec,
             scratch_shapes=[dma],
             input_output_aliases={0: 0},
             compiler_params=pltpu.CompilerParams(vmem_limit_bytes=8 * 2**20),
             name="tail",
-        )(serve_up, got, scale, norm)
+        )(serve_up, got)
         return serve_up, scale_up, serve_norm
 
     placed = (

time: 424 us -> 419 us (0.988)
  Pallas kernels: 423 us -> 417 us
    pallas_call x1, Pallas kernels: 387 us -> 369 us  [per_device(): pl.pallas_call(functools.partial(exchange_kernel, n, depth, held_back, n...]
    pallas_call x1, Pallas kernels: 21.9 us -> 33.9 us  [per_device(): pl.pallas_call(functools.partial(second_kernel, n, held_back), out_shape=...]
where the time goes in v3:
time: 419 us; the launch traced here: 418 us
  Pallas kernels  417 us (100%)
    pallas_call x1, Pallas kernels, per_device(): pl.pallas_call(functools.partial(exchange_kernel, n, depth, held_back, n...  369 us
    pallas_call x1, Pallas kernels, per_device(): pl.pallas_call(functools.partial(second_kernel, n, held_back), out_shape=...  33.9 us
    pallas_call x1, Pallas kernels, per_device(): pl.pallas_call(put_kernel, out_shape=jax.ShapeDtypeStruct((n * rows, cols...  12.3 us

profile of v3, /device:TPU:0, one launch (start us, length us, event | category | flops | bytes accessed | tf_op | source)
XLA Modules:
  0.0 418.1 jit_solution(6944191535818761372)
XLA Ops:
  0.6 369.1 %exchange.1 = (bf16[12288,1536]{1,0:T(8,128)(2,1)S(1)}, f32[1,12288]{1,0:T(1,128)}, f32[1,1536]{1,0:T(1,128)}, bf16[256,384]{1,0:T(8,128)(2,1)}, bf16[64,768]{1,0:T(8,128)(2,1)}) custom-call(bf16[1536,12288]{1,0:T(8,128)(2,1)} %w_ref.3, bf16[64,1536]{1,0:T(8,128)(2,1)} %bitcast.1, bf16[64,12288]{1,0:T(8,128)(2,1)} %high_ref.3, f32[384]{0:T(512)} %train_in.1, ...), custom_call_target="tpu_custom_call" | custom-call | tf_op jit(solution)/shard_map/exchange/pallas_call | solution.py:348
  369.7 0.0 copy-start.1
  369.7 0.0 copy-start.3
  369.7 0.0 copy-start
  369.8 0.0 copy-start.2
  369.8 12.3 %put.1.put_ref = bf16[12288,1536]{1,0:T(8,128)(2,1)} custom-call(bf16[12288,1536]{1,0:T(8,128)(2,1)S(1)} %get-tuple-element.17.held_ref), custom_call_target="tpu_custom_call" | custom-call | tf_op jit(solution)/shard_map/put/pallas_call | solution.py:373
  382.1 0.0 copy-done.1
  382.1 0.0 copy-done.3
  382.1 0.7 side.1
  382.8 0.0 copy-done
  382.8 0.0 copy-done.2
  382.8 33.9 %second.1.got_ref = bf16[768,1536]{1,0:T(8,128)(2,1)S(1)} custom-call(bf16[1536,12288]{1,0:T(8,128)(2,1)} %w_ref.3, bf16[64,768]{1,0:T(8,128)(2,1)S(1)} %copy-done.2, bf16[64,12288]{1,0:T(8,128)(2,1)S(1)} %copy-done, f32[1,1536]{1,0:T(1,128)S(1)} %copy-done.3), custom_call_target="tpu_custom_call" | custom-call | tf_op jit(solution)/shard_map/second/pallas_call | solution.py:395
  416.7 1.4 tail.1
Async XLA Ops:
  369.7 12.4 %copy-start.1 = (bf16[256,384]{1,0:T(8,128)(2,1)S(1)}, bf16[256,384]{1,0:T(8,128)(2,1)}, u32[]{:S(2)}) copy-start(bf16[256,384]{1,0:T(8,128)(2,1)} %get-tuple-element.24.norm_in) | copy-start | bytes 589828
  369.7 12.4 %copy-start.3 = (f32[1,1536]{1,0:T(1,128)S(1)}, f32[1,1536]{1,0:T(1,128)}, u32[]{:S(2)}) copy-start(f32[1,1536]{1,0:T(1,128)} %get-tuple-element.28.scale_in.scale_ref) | copy-start | bytes 18436
  369.7 13.0 %copy-start = (bf16[64,12288]{1,0:T(8,128)(2,1)S(1)}, bf16[64,12288]{1,0:T(8,128)(2,1)}, u32[]{:S(2)}) copy-start(bf16[64,12288]{1,0:T(8,128)(2,1)} %high_ref.3) | copy-start | bytes 4718596
  369.8 13.0 %copy-start.2 = (bf16[64,768]{1,0:T(8,128)(2,1)S(1)}, bf16[64,768]{1,0:T(8,128)(2,1)}, u32[]{:S(2)}) copy-start(bf16[64,768]{1,0:T(8,128)(2,1)} %get-tuple-element.27.low_ref) | copy-start | bytes 294916

commit v4 on v3

--- a/solution.py
+++ b/solution.py
@@ -168,7 +168,7 @@
     for u in range(units - held_back):
         unit_copy(u).start()
 
-    @pl.when(me % 2 == 1)
+    @pl.when(me % 2 == 0)
     def _():
         for u in range(units - held_back, units):
             unit_copy(u).start()
@@ -246,7 +246,7 @@
     for u in range(units - held_back):
         unit_copy(u).wait_send()
 
-    @pl.when(me % 2 == 1)
+    @pl.when(me % 2 == 0)
     def _():
         for u in range(units - held_back, units):
             finish_unit(u)
@@ -275,7 +275,7 @@
             device_id={"shard": me ^ far}, device_id_type=MESH,
         )
 
-    @pl.when(me % 2 == 0)
+    @pl.when(me % 2 == 1)
     def _():
         barrier = pltpu.get_barrier_semaphore()
         pl.semaphore_signal(barrier, inc=1, device_id={"shard": me ^ far}, device_id_type=MESH)
@@ -324,7 +324,7 @@
     rows = out_ref.shape[0] // n
     last = pl.ds(pl.multiple_of((me ^ (n - 2)) * rows + (rows - late), 8), late)
 
-    @pl.when(me % 2 == 0)
+    @pl.when(me % 2 == 1)
     def _():
         copy = pltpu.make_async_copy(got_ref, out_ref.at[last, :], sem)
         copy.start()

time: 419 us -> 418 us (level)
    pallas_call x1, Pallas kernels: 33.9 us -> 0.12 us  [per_device(): pl.pallas_call(functools.partial(second_kernel, n, held_back), out_shape=...]
    pallas_call x1, Pallas kernels: 369 us -> 400 us  [per_device(): pl.pallas_call(functools.partial(exchange_kernel, n, depth, held_back, n...]
where the time goes in v4:
time: 418 us; the launch traced here: 414 us
  Pallas kernels  413 us (99%)
    pallas_call x1, Pallas kernels, per_device(): pl.pallas_call(functools.partial(exchange_kernel, n, depth, held_back, n...  400 us
    pallas_call x1, Pallas kernels, per_device(): pl.pallas_call(put_kernel, out_shape=jax.ShapeDtypeStruct((n * rows, cols...  12.3 us

profile of v4, /device:TPU:0, one launch (start us, length us, event | category | flops | bytes accessed | tf_op | source)
XLA Modules:
  0.0 413.7 jit_solution(1244691034333430484)
XLA Ops:
  0.6 399.8 %exchange.1 = (bf16[12288,1536]{1,0:T(8,128)(2,1)S(1)}, f32[1,12288]{1,0:T(1,128)}, f32[1,1536]{1,0:T(1,128)}, bf16[256,384]{1,0:T(8,128)(2,1)}, bf16[64,768]{1,0:T(8,128)(2,1)}) custom-call(bf16[1536,12288]{1,0:T(8,128)(2,1)} %w_ref.3, bf16[64,1536]{1,0:T(8,128)(2,1)} %bitcast.1, bf16[64,12288]{1,0:T(8,128)(2,1)} %high_ref.3, f32[384]{0:T(512)} %train_in.1, ...), custom_call_target="tpu_custom_call" | custom-call | tf_op jit(solution)/shard_map/exchange/pallas_call | solution.py:348
  400.5 0.0 copy-start.1
  400.5 0.0 copy-start.3
  400.5 0.0 copy-start
  400.5 0.0 copy-start.2
  400.5 12.3 %put.1.put_ref = bf16[12288,1536]{1,0:T(8,128)(2,1)} custom-call(bf16[12288,1536]{1,0:T(8,128)(2,1)S(1)} %get-tuple-element.17.held_ref), custom_call_target="tpu_custom_call" | custom-call | tf_op jit(solution)/shard_map/put/pallas_call | solution.py:373
  412.9 0.0 copy-done.1
  412.9 0.0 copy-done.3
  412.9 0.7 side.1
  413.5 0.0 copy-done
  413.5 0.0 copy-done.2
  413.5 0.1 second.1.got_ref
  (1 shorter events, 0.0 us)
Async XLA Ops:
  400.5 12.4 %copy-start.1 = (bf16[256,384]{1,0:T(8,128)(2,1)S(1)}, bf16[256,384]{1,0:T(8,128)(2,1)}, u32[]{:S(2)}) copy-start(bf16[256,384]{1,0:T(8,128)(2,1)} %get-tuple-element.24.norm_in) | copy-start | bytes 589828
  400.5 12.4 %copy-start.3 = (f32[1,1536]{1,0:T(1,128)S(1)}, f32[1,1536]{1,0:T(1,128)}, u32[]{:S(2)}) copy-start(f32[1,1536]{1,0:T(1,128)} %get-tuple-element.28.scale_in.scale_ref) | copy-start | bytes 18436
  400.5 13.0 %copy-start = (bf16[64,12288]{1,0:T(8,128)(2,1)S(1)}, bf16[64,12288]{1,0:T(8,128)(2,1)}, u32[]{:S(2)}) copy-start(bf16[64,12288]{1,0:T(8,128)(2,1)} %high_ref.3) | copy-start | bytes 4718596
  400.5 13.0 %copy-start.2 = (bf16[64,768]{1,0:T(8,128)(2,1)S(1)}, bf16[64,768]{1,0:T(8,128)(2,1)}, u32[]{:S(2)}) copy-start(bf16[64,768]{1,0:T(8,128)(2,1)} %get-tuple-element.27.low_ref) | copy-start | bytes 294916
